TPU v7x, 32 devices: a whole 2x2x4 slice. The times are simulated.
32 devices in a mesh: grp: 2 (over y), shard: 16 (over z, x, core).
Axes of the slice: x: 2, y: 2, z: 4, core: 2. Of those that a mesh axis runs over, the one named last changes fastest.
Arguments:
- points: bfloat16 [65536, 128], P(('grp', 'shard')), may hold values from -9 to 9
- sub_label: int32 [65536], P(('grp', 'shard')), may hold values from 0 to 511, as said below
- block_route: int32 [512, 1], P(('grp', 'shard')), may hold values from 0 to 1; in each aligned block of 16 rows (0 to 15, 16 to 31, ...) at most 8 rows name the same one
Outputs:
- centroids: float32 [2, 512, 128], P('grp')
- min_dist: float32 [65536], P(('grp', 'shard'))
- inertia: float32 [], replicated
Inputs may be any that keep to these rules, and one draw needn't show every extreme that they name: `block_route`: of the 16 blocks of one device at most 8 name the same group. `sub_label`: A subcluster of a group may hold no points.
All inputs are finite; a program needn't handle non-finite values.
Results may differ from a plain program's by a relative error of at most 0.0003.
Values may be sent and summed in bfloat16 or wider, within the bound.
A program may use at most 64 MiB of HBM per device.

v0:
```python
import jax
import jax.numpy as jnp
from jax import lax
from jax.sharding import PartitionSpec as P

D = 128
K = 512
BLK_ROWS = 128


def block_width(total):
    for width in (512, 256, 128):
        return width
    return total


def onehot_sums(samples, labels, columns):
    total = samples.shape[0]
    width = block_width(total)
    sample_blocks = samples.reshape(total // width, width, D)
    label_blocks = labels.reshape(total // width, width)
    targets = jnp.arange(columns, dtype=jnp.int32)

    def accumulate(carry, item):
        sample_blk, label_blk = item
        onehot = (label_blk[:, None] == targets[None, :]).astype(jnp.bfloat16)
        partial_sums = lax.dot_general(
            onehot, sample_blk, (((0,), (0,)), ((), ())), preferred_element_type=jnp.float32
        )
        return (
            (carry[0] + partial_sums, carry[1] + jnp.sum(onehot.astype(jnp.float32), axis=0)),
            None,
        )

    start = (jnp.zeros((columns, D), jnp.float32), jnp.zeros((columns,), jnp.float32))
    (sums, counts), _ = lax.scan(accumulate, start, (sample_blocks, label_blocks))
    return (sums, counts)


def nearest(samples, rounded, center_norm, row_group, column_group):
    total = samples.shape[0]
    width = block_width(total)
    sample_blocks = samples.reshape(total // width, width, D)
    group_blocks = row_group.reshape(total // width, width)

    def one_block(item):
        sample_blk, group_blk = item
        cross = lax.dot_general(
            sample_blk, rounded, (((1,), (1,)), ((), ())), preferred_element_type=jnp.float32
        )
        sample_f = sample_blk.astype(jnp.float32)
        self_norm = jnp.sum(sample_f * sample_f, axis=1) / D
        dist = self_norm[:, None] - 2.0 / D * cross + center_norm[None, :]
        dist = jnp.where(group_blk[:, None] == column_group[None, :], dist, jnp.inf)
        return jnp.min(dist, axis=1)

    return lax.map(one_block, (sample_blocks, group_blocks)).reshape(-1)


def make_centers(sums, counts):
    centers = sums / jnp.maximum(counts, 1.0)[:, None]
    rounded = centers.astype(jnp.bfloat16)
    center_norm = jnp.sum(rounded.astype(jnp.float32) ** 2, axis=1) / D
    return (centers, rounded, center_norm)


def per_device(points, sub_label, block_route):
    groups = lax.axis_size("grp")
    whole_count = points.shape[0] * groups * lax.axis_size("shard")
    route = block_route[:, 0]
    row_group = jnp.repeat(route, BLK_ROWS)
    combined = row_group * K + sub_label
    sums, counts = onehot_sums(points, combined, groups * K)
    total_sums, total_counts = lax.psum((sums, counts), ("grp", "shard"))
    centers, rounded, center_norm = make_centers(total_sums, total_counts)
    column_group = jnp.arange(groups * K, dtype=jnp.int32) // K
    min_dist = nearest(points, rounded, center_norm, row_group, column_group)
    local_total = jnp.sum(min_dist)
    own_centers = lax.dynamic_slice_in_dim(
        centers.reshape(groups, K, D), lax.axis_index("grp"), 1, 0
    )
    inertia = lax.psum(local_total, ("grp", "shard")) / whole_count
    return (own_centers, min_dist, inertia)


def solution(mesh):
    placed = (P(("grp", "shard"), None), P(("grp", "shard")), P(("grp", "shard"), None))
    return jax.shard_map(
        per_device,
        mesh=mesh,
        in_specs=placed,
        out_specs=(P("grp", None, None), P(("grp", "shard")), P()),
        check_vma=False,
    )
```

profile of v0, /device:TPU:0, one launch (start us, length us, event | category | flops | bytes accessed | tf_op | source)
XLA Modules:
  0.0 206.7 jit_solution(15575715594900851412)
XLA Ops:
  7.2 0.0 all-reduce.2.cloned.1.call-start
  7.2 0.5 broadcast.49
  7.7 1.3 fusion.17
  9.1 0.8 bitcast_add_fusion
  9.8 8.8 %while.25 = (s32[]{:T(128)}, f32[1024,128]{1,0:T(8,128)S(1)}, f32[1024]{0:T(1024)S(1)}, s32[4,512]{1,0:T(4,128)S(1)}, bf16[4,512,128]{2,1,0:T(8,128)(2,1)}, /*index=5*/s32[]{:T(128)}, s32[]{:T(128)}) while((s32[]{:T(128)}, f32[1024,128]{1,0:T(8,128)S(1)}, f32[1024]{0:T(1024)S(1)}, s32[4,512]{1,0:T(4,128)S(1)}, ...), condition=%wide.region_2.3_spmd.clone, body=%wide.region_0.2_spmd.clone.sunk | while | flops 137102336 | bytes 1204828 | solution.py:36
  9.8 1.9 fusion.26
  11.7 0.3 convert_reduce_fusion.2
  12.1 1.9 fusion.26
  13.9 0.3 convert_reduce_fusion.2
  14.3 1.9 fusion.26
  16.1 0.3 convert_reduce_fusion.2
  16.5 1.9 fusion.26
  18.3 0.3 convert_reduce_fusion.2
  18.7 0.8 copy-done.1
  19.5 0.1 broadcast_in_dim.37
  19.6 0.1 broadcast_bitcast_fusion
  19.6 41.9 %psum.22 = f32[1024]{0:T(1024)S(1)} all-reduce(f32[1024]{0:T(1024)S(1)} %get-tuple-element.74), channel_id=1, replica_groups=mesh['grp'=2,'shard'=16] {'grp','shard'}, use_global_device_ids=true, to_apply=%region_4.5 | all-reduce | flops 1024 | bytes 8192 | tf_op jit(solution)/shard_map/psum | solution.py:74
  61.6 90.0 %all-reduce.2.cloned.1.call-done = f32[1024,128]{1,0:T(8,128)} async-done(((f32[1024,128]{1,0:T(8,128)}), f32[1024,128]{1,0:T(8,128)}) %all-reduce.2.cloned.1.call-update) | async-done | bytes 524304 | tf_op jit(solution)/shard_map/psum | solution.py:74
  151.5 1.4 multiply_reduce_fusion.1
  153.0 3.7 %while.24 = (s32[]{:T(128)}, f32[4,512]{1,0:T(4,128)S(1)}, s32[4,512]{1,0:T(4,128)S(1)}, bf16[4,512,128]{2,1,0:T(8,128)(2,1)S(1)}, bf16[1024,128]{1,0:T(8,128)(2...) while((s32[]{:T(128)}, f32[4,512]{1,0:T(4,128)S(1)}, s32[4,512]{1,0:T(4,128)S(1)}, ...), condition=%wide.region_9.10_spmd.clone, body=%wide.region_6.9_spmd.clone.sunk | while | flops 137567744 | bytes 557157 | solution.py:57
  153.0 0.2 multiply_reduce_fusion.3
  153.2 0.7 select_reduce_fusion.2
  153.9 0.2 multiply_reduce_fusion.3
  154.1 0.7 select_reduce_fusion.2
  154.8 0.2 multiply_reduce_fusion.3
  155.0 0.7 select_reduce_fusion.2
  155.8 0.2 multiply_reduce_fusion.3
  156.0 0.7 select_reduce_fusion.2
  156.7 0.6 reduce_sum.37
  157.3 0.6 copy.7
  157.9 39.4 %psum.23 = f32[]{:T(128)} all-reduce(f32[]{:T(128)} %reduce_sum.37), channel_id=1, replica_groups=mesh['grp'=2,'shard'=16] {'grp','shard'}, use_global_device_ids=true, to_apply=%region_11.12 | all-reduce | flops 1 | bytes 8 | tf_op jit(solution)/shard_map/psum | solution.py:82
  198.0 0.7 constant_dynamic-slice_fusion.2
  (35 shorter events, 0.4 us)
Async XLA Ops:
  7.2 144.4 %all-reduce.2.cloned.1.call-start = ((), (), s32[]{:S(2)}) async-start(), calls=%async_computation | async-start | bytes 1048576 | tf_op jit(solution)/shard_map/psum | solution.py:74
  18.6 0.8 copy-start.1
  61.6 91.4 %copy-start = (bf16[4,512,128]{2,1,0:T(8,128)(2,1)S(1)}, bf16[4,512,128]{2,1,0:T(8,128)(2,1)}, u32[]{:S(2)}) copy-start(bf16[4,512,128]{2,1,0:T(8,128)(2,1)} %get-tuple-element.251) | copy-start | bytes 1572868
Sparse Core Ops, SparseCore 0:
  19.6 131.9 all-reduce.1
where the time goes:
time: 207 us
  waiting for transfers between devices  90 us (43%)
  blocking collectives  81.3 us (39%)
  between operations  15.9 us (8%)
  matrix products  10.1 us (5%)
  other arithmetic  5.86 us (3%)
  local copies, waits for them, and re-layouts  3.08 us (1%)
    psum x1, waiting for transfers between devices, per_device(): total_sums, total_counts = lax.psum((sums, counts), ('grp', 'shard'))  90 us
    psum x1, blocking collectives, per_device(): total_sums, total_counts = lax.psum((sums, counts), ('grp', 'shard'))  41.9 us
    psum x1, blocking collectives, per_device(): inertia = lax.psum(local_total, ('grp', 'shard')) / whole_count  39.4 us
    dot_general x4, matrix products, accumulate(): lax.dot_general(onehot, sample_blk, (((0,), (0,)), ((), ())), preferred_e...  7.46 us
  transfers between devices with their start and end apart: 1, of which 1 were waited for; matrix products, arithmetic and copies ran while one was open for 0% of the time, Pallas kernels for 0%

commit v1 on v0

v1 whole, which is shorter than its diff:
```python
import functools
import math

import jax
import jax.numpy as jnp
from jax import lax
from jax.experimental import pallas as pl
from jax.experimental.pallas import tpu as pltpu
from jax.sharding import PartitionSpec as P

K = 512
MESH = pl.DeviceIdType.MESH


def plan(shard):
    cores = 2 if shard % 2 == 0 else 1
    near = 2 if (shard // cores) % 2 == 0 else 1
    rest = shard // (cores * near)
    far = math.gcd(rest, K // (cores * near) // 8)
    return cores, near, far, rest // far


def kernel(dims, route_ref, pts_ref, lab_ref, cent_ref, dist_ref, inert_ref,
           aug, onehot, acc, recv_a, recv_b, recv_c, own_d, recv_d,
           f_own, f_oth, r_own, r_oth, cn_own, cn_oth, xn, ibuf,
           sa, ra, sb, rb, sc, rc, sd, rd, sgc, rgc, sgb, rgb, sga, rga, si, ri):
    G, S, C, X, Z, O, R = dims
    n = G * S
    total_points = pts_ref.shape[0] * n
    D = pts_ref.shape[1]
    nblk, width = lab_ref.shape
    half = X * Z * R
    g = lax.axis_index("grp")
    s = lax.axis_index("shard")
    c = lax.rem(s, C)
    x = lax.rem(s // C, X)
    z = lax.rem(s // (C * X), Z)
    o = s // (C * X * Z)

    def at(g_, c_, x_, z_, o_):
        return (g_, ((o_ * Z + z_) * X + x_) * C + c_)

    def up(v, d, m):
        return lax.rem(v + d, m)

    def down(v, d, m):
        return lax.rem(v + m - d, m)

    me = g * S + s
    barrier = pltpu.get_barrier_semaphore()

    def greet(i, _):
        t = lax.rem(me + i, n)
        pl.semaphore_signal(barrier, inc=1, device_id=(t // S, lax.rem(t, S)), device_id_type=MESH)
        return 0

    lax.fori_loop(1, n, greet, 0)

    aug[:, :D] = pts_ref[...]
    aug[:, D:] = jnp.ones((pts_ref.shape[0], D), jnp.bfloat16)
    rows = G * half
    row = lax.broadcasted_iota(jnp.int32, (rows, width), 0)
    base_ids = row // half * K + lax.rem(row, half)
    eye_r = (lax.broadcasted_iota(jnp.int32, (R, D), 0) == lax.broadcasted_iota(jnp.int32, (R, D), 1))

    def local_sums(core):
        for b in range(nblk):
            lab = lab_ref[b:b + 1, :] + (route_ref[b] * K - core * half)
            onehot[:, b * width:(b + 1) * width] = jnp.where(base_ids == lab, 1.0, 0.0).astype(jnp.bfloat16)
        res = jnp.dot(onehot[...], aug[...], preferred_element_type=jnp.float32)
        cnt = jnp.where(eye_r[None], res[:, D:].reshape(G * X * Z, R, D), 0.0)
        cnt = jnp.sum(cnt, axis=1, keepdims=True)
        acc[core, :, :, :, 0:R, :] = res[:, :D].reshape(G, X, Z, R, D)
        acc[core, :, :, :, R:R + 1, :] = cnt.reshape(G, X, Z, 1, D)

    def remote(src, dst, ssem, rsem, dev):
        return pltpu.make_async_remote_copy(
            src_ref=src, dst_ref=dst, send_sem=ssem, recv_sem=rsem, device_id=dev, device_id_type=MESH)

    live = pl.ds(0, R + 1)
    sent = []

    def go(cp):
        cp.start()
        sent.append(cp)
        return cp

    oc = C - 1 - c
    if C > 1:
        local_sums(oc)
    pl.semaphore_wait(barrier, n - 1)
    if C > 1:
        cp_a = go(remote(acc.at[oc, :, :, :, live], recv_a.at[:, :, :, live], sa, ra, at(g, oc, x, z, o)))
    local_sums(c)

    if C > 1:
        cp_a.wait_recv()
        acc[c, :, :, :, 0:R + 1, :] = acc[c, :, :, :, 0:R + 1, :] + recv_a[:, :, :, 0:R + 1, :]

    plane = [(dg, dx) for dg in range(G) for dx in range(X) if dg or dx]
    plane.sort(key=lambda t: -((t[0] > 0) + (t[1] > 0)))
    cps = []
    for i, (dg, dx) in enumerate(plane):
        tg, tx = up(g, dg, G), up(x, dx, X)
        cps.append(go(remote(acc.at[c, tg, tx, :, live], recv_b.at[i, :, live], sb.at[i], rb.at[i],
                             at(tg, c, tx, z, o))))

    eye = (lax.broadcasted_iota(jnp.int32, (width, width), 0) == lax.broadcasted_iota(jnp.int32, (width, width), 1))
    for b in range(nblk):
        p = pts_ref[b * width:(b + 1) * width, :].astype(jnp.float32)
        sq = jnp.sum(p * p, axis=1, keepdims=True)
        xn[b:b + 1, :] = jnp.sum(jnp.where(eye, sq, 0.0), axis=0, keepdims=True) / D

    for cp in cps:
        cp.wait_recv()
    tot = acc[c, g, x, :, 0:R + 1, :]
    for i in range(len(plane)):
        tot = tot + recv_b[i, :, 0:R + 1, :]
    acc[c, g, x, :, 0:R + 1, :] = tot

    cps = []
    for d in sorted(range(1, Z), key=lambda d: -min(d, Z - d)):
        tz = up(z, d, Z)
        cps.append(go(remote(acc.at[c, g, x, tz, live], recv_c.at[d - 1, live], sc.at[d - 1], rc.at[d - 1],
                             at(g, c, x, tz, o))))
    for cp in cps:
        cp.wait_recv()
    tot = acc[c, g, x, z, 0:R + 1, :]
    for d in range(1, Z):
        tot = tot + recv_c[d - 1, 0:R + 1, :]
    if O > 1:
        own_d[0:R + 1, :] = tot
        cps = []
        for d in range(1, O):
            cps.append(go(remote(own_d.at[live], recv_d.at[d - 1, live], sd.at[d - 1], rd.at[d - 1],
                                 at(g, c, x, z, up(o, d, O)))))
        for cp in cps:
            cp.wait_recv()
        for d in range(1, O):
            tot = tot + recv_d[d - 1, 0:R + 1, :]
    counts = jnp.sum(jnp.where(eye_r, tot[R:R + 1, :], 0.0), axis=1, keepdims=True)
    f_own[x, z] = tot[0:R] / jnp.maximum(counts, 1.0)

    def norm(r):
        r = r.astype(jnp.float32)
        return jnp.broadcast_to(jnp.sum(r * r, axis=1, keepdims=True) / D, r.shape)

    gather_c = [None]
    for d in range(1, Z):
        gather_c.append(go(remote(f_own.at[x, z], f_own.at[x, z], sgc.at[d - 1], rgc.at[d - 1],
                                  at(g, c, x, up(z, d, Z), o))))
    gather_b = []
    gather_a = []
    for d in range(Z):
        if d:
            gather_c[d].wait_recv()
        zz = down(z, d, Z)
        rounded = f_own[x, zz].astype(jnp.bfloat16)
        r_own[g, x, zz] = rounded
        for i, (dg, dx) in enumerate(plane):
            dev = at(up(g, dg, G), c, up(x, dx, X), z, o)
            if dg:
                src, dst = r_own.at[g, x, zz], r_own.at[g, x, zz]
            else:
                src, dst = f_own.at[x, zz], f_own.at[x, zz]
            gather_b.append((d, dg, dx, go(remote(src, dst, sgb.at[d, i], rgb.at[d, i], dev))))
        if C > 1:
            gather_a.append((d, 0, 0, go(remote(f_own.at[x, zz], f_oth.at[x, zz], sga.at[d, 0], rga.at[d, 0],
                                                at(g, oc, x, z, o)))))
        cn_own[g, x, zz] = norm(rounded)
    for j, (d, dg, dx, cp) in enumerate(gather_b):
        cp.wait_recv()
        zz, gg, xx = down(z, d, Z), down(g, dg, G), down(x, dx, X)
        i = 1 + j % len(plane)
        if C > 1:
            if dg:
                src, dst = r_own.at[gg, xx, zz], r_oth.at[gg, xx, zz]
            else:
                src, dst = f_own.at[xx, zz], f_oth.at[xx, zz]
            gather_a.append((d, dg, dx, go(remote(src, dst, sga.at[d, i], rga.at[d, i], at(g, oc, x, z, o)))))
        if dg == 0:
            r_own[g, xx, zz] = f_own[xx, zz].astype(jnp.bfloat16)
        cn_own[gg, xx, zz] = norm(r_own[gg, xx, zz])

    def nearest(r_buf, cn_buf, first):
        for b in range(nblk):
            gb = route_ref[b]
            cen = r_buf[gb].reshape(half, D)
            cn = cn_buf[gb].reshape(half, D)
            cross = lax.dot_general(cen, pts_ref[b * width:(b + 1) * width, :], (((1,), (1,)), ((), ())),
                                    preferred_element_type=jnp.float32)
            low = jnp.min(cn - (2.0 / D) * cross, axis=0, keepdims=True)
            if first:
                dist_ref[b:b + 1, :] = low
            else:
                dist_ref[b:b + 1, :] = jnp.minimum(dist_ref[b:b + 1, :], low)

    nearest(r_own, cn_own, True)
    cent_ref[c] = f_own[...]
    if C > 1:
        for d, dg, dx, cp in gather_a:
            cp.wait_recv()
            zz, gg, xx = down(z, d, Z), down(g, dg, G), down(x, dx, X)
            if dg == 0:
                r_oth[g, xx, zz] = f_oth[xx, zz].astype(jnp.bfloat16)
            cn_oth[gg, xx, zz] = norm(r_oth[gg, xx, zz])
        nearest(r_oth, cn_oth, False)
    dist = dist_ref[...] + xn[...]
    dist_ref[...] = dist
    ibuf[me] = jnp.sum(dist, axis=0, keepdims=True)

    def tell(i):
        t = lax.rem(me + i, n)
        return remote(ibuf.at[me], ibuf.at[me], si.at[i], ri.at[i], (t // S, lax.rem(t, S)))

    def start(i, _):
        tell(i).start()
        return 0

    def finish(i, _):
        tell(i).wait()
        return 0

    lax.fori_loop(1, n, start, 0)
    if C > 1:
        cent_ref[oc] = f_oth[...]
    for cp in sent:
        cp.wait_send()
    lax.fori_loop(1, n, finish, 0)
    inert_ref[...] = jnp.sum(jnp.sum(ibuf[...], axis=0), axis=1, keepdims=True) / total_points


def per_device(G, S, points, sub_label, block_route):
    C, X, Z, O = plan(S)
    N, D = points.shape
    nblk = block_route.shape[0]
    width = N // nblk
    R = K // (C * X * Z)
    f32, bf16 = jnp.float32, jnp.bfloat16
    V = pltpu.VMEM
    dma = pltpu.SemaphoreType.DMA
    rp = R + 8
    peers = max(G * X - 1, 1)
    zs, os_ = max(Z - 1, 1), max(O - 1, 1)
    vmem = pl.BlockSpec(memory_space=pltpu.VMEM)
    cent, dist, inert = pl.pallas_call(
        functools.partial(kernel, (G, S, C, X, Z, O, R)),
        out_shape=(
            jax.ShapeDtypeStruct((C, X, Z, R, D), f32),
            jax.ShapeDtypeStruct((nblk, width), f32),
            jax.ShapeDtypeStruct((1, 1), f32),
        ),
        in_specs=[pl.BlockSpec(memory_space=pltpu.SMEM), vmem, vmem],
        out_specs=(vmem, vmem, vmem),
        scratch_shapes=[
            V((N, 2 * D), bf16), V((G * X * Z * R, N), bf16),
            V((C, G, X, Z, rp, D), f32), V((G, X, Z, rp, D), f32),
            V((peers, Z, rp, D), f32), V((zs, rp, D), f32),
            V((rp, D), f32), V((os_, rp, D), f32),
            V((X, Z, R, D), f32), V((X, Z, R, D), f32),
            V((G, X, Z, R, D), bf16), V((G, X, Z, R, D), bf16),
            V((G, X, Z, R, D), f32), V((G, X, Z, R, D), f32),
            V((nblk, width), f32), V((G * S, 1, width), f32),
            dma, dma, dma((peers,)), dma((peers,)), dma((zs,)), dma((zs,)),
            dma((os_,)), dma((os_,)), dma((zs,)), dma((zs,)),
            dma((Z, peers)), dma((Z, peers)), dma((Z, peers + 1)), dma((Z, peers + 1)),
            dma((G * S,)), dma((G * S,)),
        ],
        compiler_params=pltpu.CompilerParams(collective_id=0, has_side_effects=True, vmem_limit_bytes=48 * 2**20),
    )(block_route[:, 0], points, sub_label.reshape(nblk, width))
    return cent.reshape(1, K, D), dist.reshape(N), inert.reshape(())


def solution(mesh):
    placed = (P(("grp", "shard"), None), P(("grp", "shard")), P(("grp", "shard"), None))
    return jax.shard_map(
        functools.partial(per_device, mesh.shape["grp"], mesh.shape["shard"]),
        mesh=mesh,
        in_specs=placed,
        out_specs=(P("grp", None, None), P(("grp", "shard")), P()),
        check_vma=False,
    )
```

time: 207 us -> 39.2 us (0.19)
  waiting for transfers between devices: 90 us -> 0 us
  blocking collectives: 81.3 us -> 0 us
  Pallas kernels: 0 us -> 32.9 us
  between operations: 15.9 us -> 2.39 us
  matrix products: 10.1 us -> 0 us
  other arithmetic: 5.86 us -> 0 us
    psum x1 -> x0, waiting for transfers between devices: 90 us -> none  [per_device(): total_sums, total_counts = lax.psum((sums, counts), ('grp', 'shard'))]
    psum x2 -> x0, blocking collectives: 81.3 us -> none  [the longest x1 41.9 us: per_device(): total_sums, total_counts = lax.psum((sums, counts), ('grp', 'shard'))]
    pallas_call x0 -> x1, Pallas kernels: none -> 32.9 us  [per_device(): pl.pallas_call(functools.partial(kernel, (G, S, C, X, Z, O, R)), out_shap...]
    dot_general x8 -> x0, matrix products: 10.1 us -> none  [the longest x4 7.46 us: accumulate(): lax.dot_general(onehot, sample_blk, (((0,), (0,)), ((), ())), preferred_e...]
    reduce_sum x10 -> x0, other arithmetic: 3.71 us -> none  [the longest x1 1.4 us: make_centers(): center_norm = jnp.sum(rounded.astype(jnp.float32) ** 2, axis=1) / D]
  transfers between devices with their start and end apart: 1 -> 0, of which waited for: 1 -> 0; matrix products, arithmetic and copies ran while one was open for 0% -> 0% of each run, Pallas kernels for 0% -> 0%
where the time goes in v1:
time: 39.2 us; the launch traced here: 39 us
  Pallas kernels  32.9 us (84%)
  local copies, waits for them, and re-layouts  3.69 us (9%)
  between operations  2.39 us (6%)
    pallas_call x1, Pallas kernels, per_device(): pl.pallas_call(functools.partial(kernel, (G, S, C, X, Z, O, R)), out_shap...  32.9 us
    unnamed x8, local copies, waits for them, and re-layouts  3.69 us

profile of v1, /device:TPU:0, one launch (start us, length us, event | category | flops | bytes accessed | tf_op | source)
XLA Modules:
  0.0 39.0 jit_solution(17185494579286340306)
XLA Ops:
  0.6 0.0 copy-start.2
  0.6 0.6 %copy-done.2 = s32[16,1]{0,1:T(1,128)S(1)} copy-done((s32[16,1]{0,1:T(1,128)S(1)}, s32[16,1]{0,1:T(1,128)}, u32[]{:S(2)}) %copy-start.2) | copy-done | bytes 88
  1.3 0.0 copy-start
  1.3 1.0 %copy-done = bf16[2048,128]{1,0:T(8,128)(2,1)S(1)} copy-done((bf16[2048,128]{1,0:T(8,128)(2,1)S(1)}, bf16[2048,128]{1,0:T(8,128)(2,1)}, u32[]{:S(2)}) %copy-start) | copy-done | bytes 524312
  2.3 0.0 copy-start.1
  2.3 0.7 %copy-done.1 = s32[2048]{0:T(1024)S(1)} copy-done((s32[2048]{0:T(1024)S(1)}, s32[2048]{0:T(1024)}, u32[]{:S(2)}) %copy-start.1) | copy-done | bytes 8216
  3.0 32.9 %shard_map.58 = (f32[2,2,4,32,128]{4,3,2,1,0:T(8,128)S(1)}, f32[16,128]{1,0:T(8,128)S(1)}, f32[1,1]{1,0:T(1,128)}) custom-call(s32[16]{0:T(128)S(1)} %bitcast.8, bf16[2048,128]{1,0:T(8,128)(2,1)S(1)} %copy-done, s32[16,128]{1,0:T(8,128)S(1)} %bitcast.6), custom_call_target="tpu_custom_call" | custom-call | tf_op jit(solution)/shard_map/pallas_call | solution.py:246
  35.9 0.7 %copy.9 = f32[1,512,128]{2,1,0:T(8,128)} copy(f32[1,512,128]{2,1,0:T(8,128)S(1)} %bitcast.5) | data formatting | bytes 524288
  36.6 0.6 %copy.10 = f32[2048]{0:T(1024)} copy(f32[2048]{0:T(1024)S(1)} %bitcast.7) | data formatting | bytes 16384
Async XLA Ops:
  0.6 0.7 %copy-start.2 = (s32[16,1]{0,1:T(1,128)S(1)}, s32[16,1]{0,1:T(1,128)}, u32[]{:S(2)}) copy-start(s32[16,1]{0,1:T(1,128)} %param.5) | copy-start | bytes 196
  1.3 1.0 %copy-start = (bf16[2048,128]{1,0:T(8,128)(2,1)S(1)}, bf16[2048,128]{1,0:T(8,128)(2,1)}, u32[]{:S(2)}) copy-start(bf16[2048,128]{1,0:T(8,128)(2,1)} %pts_ref.1) | copy-start | bytes 1572868
  2.3 0.7 %copy-start.1 = (s32[2048]{0:T(1024)S(1)}, s32[2048]{0:T(1024)}, u32[]{:S(2)}) copy-start(s32[2048]{0:T(1024)} %param.4) | copy-start | bytes 24580
